TPU v7x, 128 devices: a whole 4x4x4 slice. The times are simulated.
128 devices in a mesh: expert: 32 (over y, x, core), dp: 4 (over z).
Axes of the slice: x: 4, y: 4, z: 4, core: 2. Of those that a mesh axis runs over, the one named last changes fastest.
Arguments:
- out_grads: bfloat16 [4, 4096, 7168], P('dp', 'expert'), may hold values from -6 to 6
- expert_ids: int32 [4, 4096, 8], P('dp', 'expert'), may hold values from 0 to 255, all different within a row; in each aligned block of 128 rows (0 to 127, 128 to 255, ..., all dimensions but the last counted through in order) at most 6 rows name the same one
- gate_probs: float32 [4, 4096, 8], P('dp', 'expert'), may hold values from 0.05 to 0.5
- hidden_acts: bfloat16 [4, 256, 192, 2048], P('dp', 'expert'), may hold values from -6 to 6
- q_previous: bfloat16 [256, 32, 7168], P('expert'), may hold values from -0.0625 to 0.0625
Outputs:
- new_basis: float32 [256, 32, 2048], P('expert')
- q_update: float32 [256, 32, 7168], P('expert', None, 'dp')
Inputs may be any that keep to these rules, and one draw needn't show every extreme that they name: `expert_ids`: each row names 8 different experts; among the rows of one device no expert is named more than 6 times.
All inputs are finite; a program needn't handle non-finite values.
Results may differ from a plain program's by a relative error of at most 0.014.
Values may be sent and summed in bfloat16 or wider, within the bound.
A program may use at most 192 MiB of HBM per device.

v0:
```python
import math

import jax
import jax.numpy as jnp
from jax import lax
from jax.sharding import PartitionSpec as P


def cut_along(shard, dim, length):
    shape = shard.shape
    blocks = shard.reshape(*shape[:dim], length, shape[dim] // length, *shape[dim + 1 :])
    return jnp.moveaxis(blocks, dim, 0)


def sent_and_summed(shard, axis, dim):
    blocks = cut_along(shard, dim, lax.axis_size(axis))
    arrived = lax.all_to_all(blocks, axis, split_axis=0, concat_axis=0, tiled=True)
    return arrived.sum(axis=0)


def copy_for_each(shard, axis):
    length = lax.axis_size(axis)
    return lax.all_to_all(
        jnp.broadcast_to(shard[None], (length, *shard.shape)), axis, 0, 0, tiled=True
    )


def of_everyone(shard, axis):
    return copy_for_each(shard, axis).astype(jnp.float32).sum(axis=0)


def in_order(blocks, dim):
    shape = list(blocks.shape[1:])
    shape[dim] *= blocks.shape[0]
    return jnp.moveaxis(blocks, 0, dim).reshape(shape)


def collect(shard, axis, dim):
    blocks = copy_for_each(shard, axis)
    return in_order(blocks, dim)


def sum_at_owner(shard, axis, dim):
    length = lax.axis_size(axis)
    blocks = lax.all_to_all(cut_along(shard, dim, length), axis, 0, 0, tiled=True)
    return jnp.sum(blocks.astype(jnp.float32), axis=0)


def slot_tables(route_ids, gate_values, num_experts, capacity):
    flat_ids = route_ids.reshape(-1)
    row_count = flat_ids.shape[0]
    top_k = route_ids.shape[-1]
    one_hot = (flat_ids[:, None] == jnp.arange(num_experts, dtype=jnp.int32)[None, :]).astype(
        jnp.int32
    )
    earlier = jnp.cumsum(one_hot, axis=0) - one_hot
    position = jnp.sum(earlier * one_hot, axis=1)
    slot_index = flat_ids * capacity + position
    token_of = (
        jnp.zeros((num_experts * capacity,), jnp.int32)
        .at[slot_index]
        .set(jnp.arange(row_count, dtype=jnp.int32) // top_k)
    )
    gate_of = (
        jnp.zeros((num_experts * capacity,), jnp.float32)
        .at[slot_index]
        .set(gate_values.reshape(-1))
    )
    return (token_of, gate_of)


def first_factor(arrived, q_part, hidden_part):
    mixed = jnp.einsum(
        "sjcd,jrd->jscr", arrived, q_part, preferred_element_type=jnp.float32
    ).astype(jnp.bfloat16)
    return jnp.einsum("jscr,jscf->jrf", mixed, hidden_part, preferred_element_type=jnp.float32)


def second_factor(arrived, projected):
    return jnp.einsum("jscr,sjcd->jrd", projected, arrived, preferred_element_type=jnp.float32)


def lower_inverse(gram):
    lower = jnp.linalg.cholesky(gram)
    identity = jnp.broadcast_to(jnp.eye(gram.shape[1], dtype=jnp.float32), gram.shape)
    return jax.vmap(lambda left, right: jax.scipy.linalg.solve_triangular(left, right, lower=True))(
        lower, identity
    )


def gram_of(values):
    return jnp.einsum("jrf,jsf->jrs", values, values)


def apply_inverse(inverse, values):
    return jnp.einsum("jrs,jsf->jrf", inverse, values)


def local(out_grads, expert_ids, gate_probs, hidden_acts, q_previous):
    n_expert = lax.axis_size("expert")
    local_count = hidden_acts.shape[1]
    slot_count = hidden_acts.shape[2]
    capacity = slot_count // n_expert
    width = out_grads.shape[2]
    token_of, gate_of = slot_tables(expert_ids[0], gate_probs[0], local_count * n_expert, capacity)
    picked = jnp.take(out_grads[0], token_of, axis=0)
    routed = (picked.astype(jnp.float32) * gate_of[:, None]).astype(jnp.bfloat16)
    routed = routed.reshape(n_expert, local_count, capacity, width)
    hidden_blocks = hidden_acts[0].reshape(local_count, n_expert, capacity, hidden_acts.shape[3])
    arrived = lax.all_to_all(routed, "expert", split_axis=0, concat_axis=0, tiled=True)
    factor = first_factor(arrived, q_previous, hidden_blocks)
    share = sent_and_summed(factor, "dp", 2)
    gram = of_everyone(gram_of(share).astype(jnp.bfloat16), "dp").astype(jnp.float32)
    inverse = lower_inverse(gram)
    ortho = collect(apply_inverse(inverse, share).astype(jnp.bfloat16), "dp", 2).astype(jnp.float32)
    ortho_half = ortho.astype(jnp.bfloat16)
    projected = jnp.einsum(
        "jscf,jrf->jscr", hidden_blocks, ortho_half, preferred_element_type=jnp.float32
    ).astype(jnp.bfloat16)
    terms = second_factor(arrived, projected)
    q_update = sum_at_owner(terms.astype(jnp.bfloat16), "dp", 2)
    new_basis = ortho * math.sqrt(ortho.shape[2])
    return (new_basis, q_update)


def solution(mesh):
    return jax.shard_map(
        local,
        mesh=mesh,
        in_specs=(
            P("dp", "expert", None),
            P("dp", "expert", None),
            P("dp", "expert", None),
            P("dp", "expert", None, None),
            P("expert", None, None),
        ),
        out_specs=(P("expert", None, None), P("expert", None, "dp")),
        check_vma=False,
    )
```

profile of v0, /device:TPU:6, one launch (start us, length us, event | category | flops | bytes accessed | tf_op | source)
XLA Modules:
  0.0 630.6 jit_solution(4050087780140486832)
XLA Ops:
  0.6 0.0 copy-start
  0.6 0.9 copy.57
  1.6 0.1 eq.30
  1.7 0.1 eq.26
  1.8 0.7 broadcast_multiply_fusion
  2.4 0.1 copy.59
  2.5 0.2 fusion.29
  2.8 0.1 broadcast_add_fusion
  2.9 0.3 copy.60
  3.2 0.1 copy.56
  3.3 0.1 mul.38
  3.4 0.4 fusion.27
  3.8 4.3 scatter_custom_fusion
  8.2 0.0 copy-done
  8.2 16.4 %gather_fusion = bf16[1536,7168]{1,0:T(8,128)(2,1)} fusion(bf16[128,7168]{1,0:T(8,128)(2,1)S(1)} %bitcast.65, s32[2048]{0:T(1024)S(1)} %pad_clamp_fusion), kind=kCustom, calls=%fused_computation | custom fusion | bytes 44046336 | tf_op jit(solution)/shard_map/jit(_take)/gather | solution.py:106
  24.6 0.0 copy-start.3
  24.6 30.7 %gather.7 = bf16[32,8,6,7168]{3,2,1,0:T(8,128)(2,1)} reshape(bf16[1536,7168]{1,0:T(8,128)(2,1)} %gather_fusion) | data formatting | bytes 44040192 | tf_op jit(solution)/shard_map/jit(_take)/gather | solution.py:106
  55.3 0.2 broadcast_in_dim.44
  55.5 0.0 copy-done.3
  55.5 0.1 copy.61
  55.6 0.1 reshape.113
  55.7 4.3 scatter_custom_fusion.1
  60.0 0.1 mul.40
  60.2 20.4 %multiply_convert_fusion = bf16[32,8,6,7168]{3,2,1,0:T(8,128)(2,1)} fusion(f32[32,8,6]{2,1,0:T(8,128)S(1)} %mul.40, bf16[32,8,6,7168]{3,2,1,0:T(8,128)(2,1)} %gather.7, pred[32,8,6]{2,1,0:T(8,128)(4,1)S(1)} %broadcast_in_dim.44), kind=kLoop, calls=%fused_computation.3 | loop fusion | flops 44040192 | bytes 44047872 | tf_op jit(solution)/shard_map/convert_element_type | solution.py:107
  80.5 25.2 %copy.62 = bf16[32,8,6,7168]{3,1,2,0:T(8,128)(2,1)} copy(bf16[32,8,6,7168]{3,2,1,0:T(8,128)(2,1)} %multiply_convert_fusion) | data formatting | bytes 44040192 | tf_op jit(solution)/shard_map/convert_element_type | solution.py:107
  105.7 8.0 %all-to-all-start = ((bf16[32,8,6,7168]{3,1,2,0:T(8,128)(2,1)}), bf16[32,8,6,7168]{3,1,2,0:T(8,128)(2,1)}, u32[]{:S(2)}, u32[]{:S(2)}) async-start(bf16[32,8,6,7168]{3,1,2,0:T(8,128)(2,1)} %copy.62), calls=%async_computation | async-start | bytes 44040192 | tf_op jit(solution)/shard_map/all_to_all | solution.py:110
  113.7 9.0 %copy.64 = bf16[1,8,192,2048]{3,1,2,0:T(8,128)(2,1)} copy(bf16[1,8,192,2048]{3,2,1,0:T(8,128)(2,1)} %param.8) | data formatting | bytes 12582912 | tf_op args[3]
  122.7 266.2 %all-to-all-done = bf16[32,8,6,7168]{3,1,2,0:T(8,128)(2,1)} async-done(((bf16[32,8,6,7168]{3,1,2,0:T(8,128)(2,1)}), bf16[32,8,6,7168]{3,1,2,0:T(8,128)(2,1)}, u32[]{:S(2)}, u32[]{:S(2)}) %all-to-all-start) | async-done | bytes 22020128 | tf_op jit(solution)/shard_map/all_to_all | solution.py:110
  388.9 0.0 copy-start.2
  388.9 22.8 %fusion.18 = bf16[8,32,6,32]{3,1,2,0:T(8,128)(2,1)S(1)} fusion(bf16[8,32,7168]{2,1,0:T(8,128)(2,1)} %param.9, bf16[32,8,6,7168]{3,1,2,0:T(8,128)(2,1)} %all-to-all-done), kind=kOutput, calls=%fused_computation.20 | convolution fusion | flops 704692224 | bytes 25788416 | tf_op jit(solution)/shard_map/sjcd,jrd->jscr/dot_general | solution.py:73
  411.6 0.0 copy-done.2
  411.6 7.0 %fusion.12 = f32[8,32,2048,1]{2,1,3,0:T(8,128)S(1)} fusion(bf16[8,32,6,32]{3,1,2,0:T(8,128)(2,1)S(1)} %fusion.18, bf16[8,32,6,2048]{3,0,2,1:T(8,128)(2,1)S(1)} %bitcast.68), kind=kOutput, calls=%fused_computation.13 | convolution fusion | flops 201326592 | bytes 8486912 | tf_op jit(solution)/shard_map/jscr,jscf->jrf/dot_general | solution.py:76
  418.6 1.6 copy.104
  420.2 5.3 all-to-all-start.1
  425.5 26.5 %all-to-all-done.1 = f32[4,8,32,512]{3,2,1,0:T(8,128)} async-done(((f32[4,8,32,512]{3,2,1,0:T(8,128)}), f32[4,8,32,512]{3,2,1,0:T(8,128)}, u32[]{:S(2)}, u32[]{:S(2)}) %all-to-all-start.1) | async-done | bytes 2097184 | tf_op jit(solution)/shard_map/all_to_all | solution.py:17
  452.0 1.8 reduce_sum.40
  453.9 0.2 fusion.45
  454.1 0.9 reshape.127
  455.1 3.3 all-to-all-start.2
  458.4 5.8 all-to-all-done.2
  464.1 0.2 reshape.128
  464.3 0.1 convert_reduce_fusion.1
  464.4 0.1 copy.68
  464.5 23.4 %custom-call.8 = f32[8,32,32]{2,1,0:T(8,128)S(1)} custom-call(f32[8,32,32]{2,1,0:T(8,128)S(1)} %fusion.34), custom_call_target="Cholesky" | custom-call | tf_op jit(solution)/shard_map/jit(cholesky)/cholesky | solution.py:84
  488.0 0.1 compare_reduce_fusion
  488.1 0.1 select_bitcast_fusion
  488.2 19.7 %custom-call.9 = f32[8,1,32,32]{2,3,1,0:T(8,128)S(1)} custom-call(f32[8,1,32,32]{3,2,1,0:T(8,128)S(1)} %select_bitcast_fusion), custom_call_target="InvertDiagBlocksLowerTriangular" | custom-call | tf_op jit(solution)/shard_map/vmap(jit(_solve_triangular))/triangular_solve | solution.py:86
  507.9 0.4 fusion.32
  508.3 0.2 fusion.44
  508.5 0.1 broadcast_in_dim.51
  508.6 18.5 %all_to_all.25 = bf16[4,8,32,512]{3,2,1,0:T(8,128)(2,1)S(1)} all-to-all(bf16[4,8,32,512]{3,2,1,0:T(8,128)(2,1)S(1)} %broadcast_in_dim.51), channel_id=1, replica_groups=mesh['expert'=32,'dp'=4] {'dp'}, dimensions={0} | all-to-all | bytes 2097152 | tf_op jit(solution)/shard_map/all_to_all | solution.py:23
  527.2 0.8 copy.70
  528.0 1.6 reshape.120
  529.6 10.3 %fusion.23 = bf16[8,32,6,32]{1,3,2,0:T(8,128)(2,1)S(1)} fusion(bf16[8,32,6,2048]{3,0,2,1:T(8,128)(2,1)} %bitcast.67, bf16[8,32,2048,1]{2,1,0,3:T(8,128)(2,1)} %reshape.120), kind=kOutput, calls=%fused_computation.21 | convolution fusion | flops 201375744 | bytes 7438336 | tf_op jit(solution)/shard_map/jscf,jrf->jscr/dot_general | solution.py:117
  539.9 36.5 %fusion.7 = bf16[8,32,7168]{2,1,0:T(8,128)(2,1)S(1)} fusion(bf16[8,32,6,32]{1,3,2,0:T(8,128)(2,1)S(1)} %fusion.23, bf16[32,8,6,7168]{3,1,2,0:T(8,128)(2,1)} %all-to-all-done), kind=kOutput, calls=%fused_computation.9 | convolution fusion | flops 706478080 | bytes 25788416 | tf_op jit(solution)/shard_map/jscr,sjcd->jrd/dot_general | solution.py:80
  576.4 2.3 copy.103
  578.7 4.7 all-to-all-start.4
  583.5 0.0 copy-start.1
  583.5 0.1 copy.82
  583.6 1.6 convert_multiply_fusion
  585.2 41.2 %all-to-all-done.4 = bf16[4,8,32,1792]{3,2,1,0:T(8,128)(2,1)} async-done(((bf16[4,8,32,1792]{3,2,1,0:T(8,128)(2,1)}), bf16[4,8,32,1792]{3,2,1,0:T(8,128)(2,1)}, u32[]{:S(2)}, u32[]{:S(2)}) %all-to-all-start.4) | async-done | bytes 3670048 | tf_op jit(solution)/shard_map/all_to_all | solution.py:45
  626.4 4.0 convert_reduce_fusion
  630.4 0.0 copy-done.1
  (14 shorter events, 0.2 us)
Async XLA Ops:
  0.6 7.6 %copy-start = (bf16[1,128,7168]{2,1,0:T(8,128)(2,1)S(1)}, bf16[1,128,7168]{2,1,0:T(8,128)(2,1)}, u32[]{:S(2)}) copy-start(bf16[1,128,7168]{2,1,0:T(8,128)(2,1)} %param.5) | copy-start | bytes 5505028
  24.6 30.9 %copy-start.3 = (f32[1,128,8]{1,2,0:T(8,128)S(1)}, f32[1,128,8]{1,2,0:T(8,128)}, u32[]{:S(2)}) copy-start(f32[1,128,8]{1,2,0:T(8,128)} %param.7) | copy-start | bytes 12292
  105.7 283.1 %all-to-all-start = ((bf16[32,8,6,7168]{3,1,2,0:T(8,128)(2,1)}), bf16[32,8,6,7168]{3,1,2,0:T(8,128)(2,1)}, u32[]{:S(2)}, u32[]{:S(2)}) async-start(bf16[32,8,6,7168]{3,1,2,0:T(8,128)(2,1)} %copy.62), calls=%async_computation | async-start | bytes 44040192 | tf_op jit(solution)/shard_map/all_to_all | solution.py:110
  388.9 22.8 %copy-start.2 = (bf16[1,8,192,2048]{3,1,2,0:T(8,128)(2,1)S(1)}, bf16[1,8,192,2048]{3,1,2,0:T(8,128)(2,1)}, u32[]{:S(2)}) copy-start(bf16[1,8,192,2048]{3,1,2,0:T(8,128)(2,1)} %copy.64) | copy-start | bytes 18874372
  420.2 31.8 %all-to-all-start.1 = ((f32[4,8,32,512]{3,2,1,0:T(8,128)}), f32[4,8,32,512]{3,2,1,0:T(8,128)}, u32[]{:S(2)}, u32[]{:S(2)}) async-start(f32[4,8,32,512]{3,2,1,0:T(8,128)} %bitcast.72), calls=%async_computation.1 | async-start | bytes 4194304 | tf_op jit(solution)/shard_map/all_to_all | solution.py:17
  455.1 9.1 %all-to-all-start.2 = ((bf16[4,2,4096]{2,1,0:T(2,128)(2,1)}), bf16[4,2,4096]{2,1,0:T(2,128)(2,1)S(1)}, u32[]{:S(2)}, u32[]{:S(2)}) async-start(bf16[4,2,4096]{2,1,0:T(2,128)(2,1)} %reshape.127), calls=%async_computation.2 | async-start | bytes 131072 | tf_op jit(solution)/shard_map/all_to_all | solution.py:23
  578.7 47.7 %all-to-all-start.4 = ((bf16[4,8,32,1792]{3,2,1,0:T(8,128)(2,1)}), bf16[4,8,32,1792]{3,2,1,0:T(8,128)(2,1)}, u32[]{:S(2)}, u32[]{:S(2)}) async-start(bf16[4,8,32,1792]{3,2,1,0:T(8,128)(2,1)} %bitcast.69), calls=%async_computation.4 | async-start | bytes 7340032 | tf_op jit(solution)/shard_map/all_to_all | solution.py:45
  583.5 47.0 %copy-start.1 = (bf16[1,128,7168]{2,1,0:T(8,128)(2,1)S(1)}, bf16[1,128,7168]{2,1,0:T(8,128)(2,1)}, u32[]{:S(2)}) copy-start(bf16[1,128,7168]{2,1,0:T(8,128)(2,1)} %param.5) | copy-start | bytes 5505028
where the time goes:
time: 639 us; the launch traced here: 631 us
  waiting for transfers between devices  340 us (53%)
  local copies, waits for them, and re-layouts  99.9 us (16%)
  matrix products  77.4 us (12%)
  other arithmetic  72.7 us (11%)
  starting transfers between devices  21.3 us (3%)
  blocking collectives  18.5 us (3%)
    all_to_all x1, waiting for transfers between devices, local(): lax.all_to_all(routed, 'expert', split_axis=0, concat_axis=0, tiled=True)  266 us
    gather x2, local copies, waits for them, and re-layouts, local(): picked = jnp.take(out_grads[0], token_of, axis=0)  47.1 us
    all_to_all x1, waiting for transfers between devices, sum_at_owner(): lax.all_to_all(cut_along(shard, dim, length), axis, 0, 0, tiled=True)  41.2 us
    dot_general x1, matrix products, second_factor(): jnp.einsum('jscr,sjcd->jrd', projected, arrived, preferred_element_type=j...  36.5 us
    all_to_all x1, waiting for transfers between devices, sent_and_summed(): lax.all_to_all(blocks, axis, split_axis=0, concat_axis=0, tiled=True)  26.5 us
    convert_element_type x1, local copies, waits for them, and re-layouts, local(): (picked.astype(jnp.float32) * gate_of[:, None]).astype(jnp.bfloat16)  25.2 us
    another operation x4, other arithmetic, lower_inverse(): lower = jnp.linalg.cholesky(gram)  23.6 us
    dot_general x1, matrix products, first_factor(): jnp.einsum('sjcd,jrd->jscr', arrived, q_part, preferred_element_type=jnp....  22.8 us
  transfers between devices with their start and end apart: 4, of which 4 were waited for; matrix products, arithmetic and copies ran while one was open for 2% of the time, Pallas kernels for 0%

commit v1 on v0

v1 whole, which is shorter than its diff:
```python
import math

import jax
import jax.numpy as jnp
from jax import lax
from jax.experimental import pallas as pl
from jax.experimental.pallas import tpu as pltpu
from jax.sharding import PartitionSpec as P

MESH = pl.DeviceIdType.MESH
BF, F32 = jnp.bfloat16, jnp.float32
HI = lax.Precision.HIGHEST
SLOT = 8
CAP = 6


def dot_nt(left, right, **more):
    return lax.dot_general(left, right, (((1,), (1,)), ((), ())), preferred_element_type=F32, **more)


def dot_nn(left, right, **more):
    return lax.dot_general(left, right, (((1,), (0,)), ((), ())), preferred_element_type=F32, **more)


def dot_tn(left, right, **more):
    return lax.dot_general(left, right, (((0,), (0,)), ((), ())), preferred_element_type=F32, **more)


def iota(shape, dim):
    return lax.broadcasted_iota(jnp.int32, shape, dim)


def slot_selection():
    row, slot = iota((256, 192), 0), iota((256, 192), 1)
    x, y, core, place = row // 64, (row // 16) % 4, (row // 8) % 2, row % 8
    at = ((y * 4 + x) * 2 + core) * CAP + place
    return jnp.where((at == slot) & (place < CAP), 1.0, 0.0).astype(BF)


def kernel(
    ids_ref, gates_ref, grads_ref, hidden_ref, prev_ref, basis_ref, update_ref,
    tok, meta, q_row, routed, pick, gate_col, hid, m_out, m_in, m_t, f_out, f_in, fac, orth, p_out, p_in,
    load_sem, zs, zr, as_, ar, hs, hr, ps, pr,
    mzs, mzr, mas, mar, mhs, mhr, mps, mpr,
    qs, qr, ms, mr, fs, fr, os_, or_, js, jr, us, ur,
):
    width = tok.shape[2]
    e, z = lax.axis_index("expert"), lax.axis_index("dp")
    y, x, c = e // 8, (e // 2) % 4, e % 2

    def dev(yy, xx, cc, zz):
        return {"expert": (yy * 4 + xx) * 2 + cc, "dp": zz}

    def turn(v, by):
        return lax.rem(v + by, 4)

    def copy(src, dst, send, recv, device):
        return pltpu.make_async_remote_copy(src, dst, send, recv, device_id=device, device_id_type=MESH)

    def block(zz, yy, cc):
        return (zz * 4 + yy) * 2 + cc

    cols = lambda zz: pl.ds(pl.multiple_of(zz * width, 128), width)

    own = block(z, y, c)
    load_tok = pltpu.make_async_copy(grads_ref.at[:, cols(z)], tok.at[own], load_sem.at[0])
    load_q = pltpu.make_async_copy(prev_ref.at[:, cols(z)], q_row.at[x], load_sem.at[1])
    load_hid = pltpu.make_async_copy(hidden_ref, hid, load_sem.at[2])
    load_tok.start()
    load_q.start()
    load_hid.start()

    barrier = pltpu.get_barrier_semaphore()
    peers = [dev(turn(y, 1), x, c, z), dev(turn(y, 3), x, c, z), dev(y, x, 1 - c, z)]
    for bx in range(4):
        for bz in range(4):
            if bx or bz:
                peers.append(dev(y, turn(x, bx), c, turn(z, bz)))
    for peer in peers:
        pl.semaphore_signal(barrier, inc=1, device_id=peer, device_id_type=MESH)

    ids = ids_ref[...]
    expert_row = iota((256, 128), 0)
    named = jnp.zeros((256, 128), F32)
    for k in range(8):
        named = named + jnp.where(ids[k : k + 1, :] == expert_row, 1.0, 0.0)
    before = jnp.where(iota((128, 128), 0) < iota((128, 128), 1), 1.0, 0.0).astype(BF)
    earlier = dot_nn(named.astype(BF), before)
    place = jnp.concatenate(
        [
            jnp.sum(jnp.where(ids[k : k + 1, :] == expert_row, earlier, 0.0), axis=0, keepdims=True)
            for k in range(8)
        ],
        axis=0,
    )
    holder, inner = ids // 8, ids % 8
    group = (holder // 8) * 2 + holder % 2
    base = group * 512 + ((holder // 2) % 4) * 128 + inner * 16
    meta[own, 0:8, :] = base.astype(F32) + place
    meta[own, 8:16, :] = gates_ref[...]

    pl.semaphore_wait(barrier, len(peers))

    waits = []

    def go(cp):
        cp.start()
        waits.append(cp)

    zorder = [0, 1, 3, 2]
    for r in (1, 3, 2):
        to = turn(z, r)
        go(copy(meta.at[own], meta.at[own], mzs.at[r], mzr.at[r], dev(y, x, c, to)))
        go(copy(grads_ref.at[:, cols(to)], tok.at[own], zs.at[r], zr.at[r], dev(y, x, c, to)))
    load_q.wait()
    for r in (2, 1, 3):
        go(copy(q_row.at[x], q_row.at[x], qs.at[r], qr.at[r], dev(y, turn(x, r), c, z)))
    load_tok.wait()

    up, down, partner = dev(turn(y, 1), x, c, z), dev(turn(y, 3), x, c, z), dev(y, x, 1 - c, z)

    def to_partner(k, zz, dy):
        b = block(zz, turn(y, dy), c)
        go(copy(meta.at[b], meta.at[b], mps.at[k, dy], mpr.at[k, dy], partner))
        go(copy(tok.at[b], tok.at[b], ps.at[k, dy], pr.at[k, dy], partner))

    def source(k):
        return turn(z, zorder[k])

    def stage_a(k):
        zz = source(k)
        b = block(zz, y, c)
        if k:
            r = (4 - zorder[k]) % 4
            copy(meta.at[b], meta.at[b], mzs.at[r], mzr.at[r], up).wait_recv()
            copy(tok.at[b], tok.at[b], zs.at[r], zr.at[r], up).wait_recv()
        for way, device in ((0, up), (1, down)):
            go(copy(meta.at[b], meta.at[b], mas.at[way, k], mar.at[way, k], device))
            go(copy(tok.at[b], tok.at[b], as_.at[way, k], ar.at[way, k], device))
        to_partner(k, zz, 0)

    def stage_b(k):
        zz = source(k)
        for way, device, dy in ((0, up, 3), (1, down, 1)):
            b = block(zz, turn(y, dy), c)
            copy(meta.at[b], meta.at[b], mas.at[way, k], mar.at[way, k], device).wait_recv()
            copy(tok.at[b], tok.at[b], as_.at[way, k], ar.at[way, k], device).wait_recv()
            half = pl.ds(way * 64, 64)
            if way == 0:
                go(copy(meta.at[b], meta.at[b], mhs.at[k], mhr.at[k], device))
            go(copy(tok.at[b, half], tok.at[b, half], hs.at[way, k], hr.at[way, k], device))
            to_partner(k, zz, dy)

    def stage_h(k):
        zz = source(k)
        b = block(zz, turn(y, 2), c)
        copy(meta.at[b], meta.at[b], mhs.at[k], mhr.at[k], up).wait_recv()
        for way in range(2):
            half = pl.ds(way * 64, 64)
            copy(tok.at[b, half], tok.at[b, half], hs.at[way, k], hr.at[way, k], up).wait_recv()
        to_partner(k, zz, 2)

    mine = ((y * 2 + c) * 512).astype(F32)
    row_of = iota((512, 128), 0).astype(F32)

    def rows_of(zz, yy):
        pair = zz * 4 + yy
        gates = []
        for cc in range(2):
            info = meta[pair * 2 + cc]
            want = info[0:8] - mine + float(cc * 8)
            gate = jnp.zeros((512, 128), F32)
            for k in range(8):
                gate = jnp.where(row_of == want[k : k + 1], info[8 + k : 9 + k], gate)
            gates.append(gate)
            pick[:, cc * 128 : cc * 128 + 128] = jnp.where(gate > 0.0, 1.0, 0.0).astype(BF)
        gate_col[...] = jnp.broadcast_to(
            jnp.sum(gates[0] + gates[1], axis=1, keepdims=True), gate_col.shape
        )
        to = pl.ds(pl.multiple_of(pair * 16, 16), 16)

        @pl.loop(0, width // 256)
        def _(n):
            at = pl.ds(pl.multiple_of(n * 256, 256), 256)
            rows = jnp.concatenate([tok[pair * 2, :, at], tok[pair * 2 + 1, :, at]], axis=0)
            got = dot_nn(pick[...], rows)
            gate = gate_col[...]
            got = got * jnp.concatenate([gate, gate], axis=1)
            routed[:, to, at] = got.astype(BF).reshape(32, 16, 256)

    lane_expert = iota((64, 256), 1) // 32

    def stage_c(k):
        zz = source(k)
        for dy in range(4):
            b = block(zz, turn(y, dy), 1 - c)
            copy(meta.at[b], meta.at[b], mps.at[k, dy], mpr.at[k, dy], partner).wait_recv()
            copy(tok.at[b], tok.at[b], ps.at[k, dy], pr.at[k, dy], partner).wait_recv()

        @pl.loop(0, 4)
        def _(i):
            rows_of(zz, i)

        part = pl.ds(pl.multiple_of(zz * 64, 64), 64)
        if k == 0:
            for r in (1, 2, 3):
                b = turn(x, 4 - r)
                copy(q_row.at[b], q_row.at[b], qs.at[r], qr.at[r], up).wait_recv()
        for r in range(4):
            to = turn(x, r)
            rows = routed[pl.ds(to * 8, 8), part, :].reshape(512, width)
            every = dot_nt(rows, q_row[to])
            total = jnp.zeros((64, 256), F32)
            for j in range(8):
                total = total + jnp.where(lane_expert == j, every[j * 64 : j * 64 + 64], 0.0)
            if k == 0 and r == 0:
                m_in[0, 0] = total.astype(BF)
            else:
                m_out[k, r] = total.astype(BF)
                go(
                    copy(
                        m_out.at[k, r],
                        m_in.at[r, k],
                        ms.at[k, r],
                        mr.at[k, r],
                        dev(y, to, c, zz),
                    )
                )

    stage_a(0)
    stage_a(1)
    stage_b(0)
    stage_a(2)
    stage_h(0)
    stage_b(1)
    stage_c(0)
    stage_a(3)
    stage_h(1)
    stage_b(2)
    stage_c(1)
    stage_h(2)
    stage_b(3)
    stage_c(2)
    stage_h(3)
    stage_c(3)

    while waits:
        waits.pop(0).wait_send()

    load_hid.wait()
    parts = []
    for r in range(4):
        total = None
        for k in range(4):
            if k or r:
                copy(m_out.at[k, r], m_in.at[r, k], ms.at[k, r], mr.at[k, r], up).wait_recv()
            got = m_in[r, k].astype(F32)
            total = got if total is None else total + got
        parts.append(total.astype(BF))
    raw = jnp.concatenate(parts, axis=0)

    def selection():
        row, slot = iota((256, 192), 0), iota((256, 192), 1)
        from_x = (x + 4 - row // 64) % 4
        at = ((((row // 16) % 4) * 4 + from_x) * 2 + (row // 8) % 2) * CAP + row % 8
        return jnp.where((at == slot) & (row % 8 < CAP), 1.0, 0.0).astype(BF)

    select = selection()
    m_t[...] = dot_tn(raw, select).astype(BF)

    for k, r in enumerate((2, 1, 3, 0)):
        to = turn(z, r)
        for i in range(2):
            j = to * 2 + i
            rows = m_t[pl.ds(pl.multiple_of(j * 32, 32), 32), :]
            got = dot_nn(rows, hid[j])
            if r:
                f_out[r, i * 32 : i * 32 + 32, :] = got.astype(BF)
            else:
                fac[i * 32 : i * 32 + 32, :] = got
        if r:
            go(copy(f_out.at[r], f_in.at[r], fs.at[r], fr.at[r], dev(y, x, c, to)))
    total = fac[0:64, :]
    for r in (1, 3, 2):
        copy(f_out.at[r], f_in.at[r], fs.at[r], fr.at[r], up).wait_recv()
        total = total + f_in[r].astype(F32)
    fac[0:64, :] = total
    fac[64:128, :] = total

    gram = dot_nt(fac[0:64, :], fac[...], precision=HI)
    lane, row = iota((32, 128), 1), iota((32, 128), 0)
    eye = jnp.where(lane % 32 == row, 1.0, 0.0)
    work = jnp.where(lane >= 96, gram[32:64], jnp.where(lane >= 64, gram[0:32], eye))
    first = (lane // 32) % 2 == 0
    for k in range(32):
        one = jnp.sum(jnp.where(lane == 64 + k, work, 0.0), axis=1, keepdims=True)
        two = jnp.sum(jnp.where(lane == 96 + k, work, 0.0), axis=1, keepdims=True)
        one = one / one[k : k + 1, :]
        two = two / two[k : k + 1, :]
        factor = jnp.where(row > k, jnp.where(first, one, two), 0.0)
        work = work - factor * work[k : k + 1, :]
    one = jnp.sum(jnp.where(lane == 64 + row, work, 0.0), axis=1, keepdims=True)
    two = jnp.sum(jnp.where(lane == 96 + row, work, 0.0), axis=1, keepdims=True)
    work = work * jnp.where(first, 1.0 / jnp.sqrt(one), 1.0 / jnp.sqrt(two))
    inverse = jnp.concatenate(
        [jnp.where(lane < 32, work, 0.0), jnp.where((lane >= 32) & (lane < 64), work, 0.0)], axis=0
    )
    ortho = dot_nn(inverse[:, 0:64], fac[0:64, :], precision=HI)
    orth[z] = ortho.astype(BF)
    for r in (2, 1, 3):
        go(copy(orth.at[z], orth.at[z], os_.at[r], or_.at[r], dev(y, x, c, turn(z, r))))

    root = math.sqrt(hid.shape[2])
    for r in (0, 1, 3, 2):
        zz = turn(z, 4 - r)
        if r:
            copy(orth.at[zz], orth.at[zz], os_.at[r], or_.at[r], up).wait_recv()
        for i in range(2):
            j = zz * 2 + i
            got = dot_nt(orth[zz, i * 32 : i * 32 + 32, :], hid[j])
            m_t[pl.ds(pl.multiple_of(j * 32, 32), 32), :] = got.astype(BF)
    spread = dot_nt(select, m_t[...]).astype(BF)
    for r in range(4):
        p_out[r] = spread[r * 64 : r * 64 + 64]
    for r in (2, 1, 3, 0):
        for q in (2, 1, 3, 0):
            if r or q:
                go(
                    copy(
                        p_out.at[r],
                        p_in.at[r, z],
                        js.at[r, q],
                        jr.at[r, q],
                        dev(y, turn(x, 4 - r), c, turn(z, q)),
                    )
                )
    p_in[0, z] = spread[0:64]
    for zz in range(4):
        basis_ref[zz * 64 : zz * 64 + 64, :] = orth[zz].astype(F32) * root

    for r in (2, 1, 3, 0):
        b = turn(x, r)
        for q in range(4):
            if r or q:
                zz = turn(z, 4 - q)
                copy(p_out.at[r], p_in.at[r, zz], js.at[r, q], jr.at[r, q], up).wait_recv()
        terms = jnp.concatenate([p_in[r, zz] for zz in range(4)], axis=0)
        pick[0:256, :] = terms.astype(F32).T.astype(BF)

        @pl.loop(0, 8)
        def _(j):
            at = pl.ds(pl.multiple_of(j * 32, 32), 32)
            got = dot_nn(pick[at, :], routed[b * 8 + j])
            if r:
                to = pl.ds(pl.multiple_of((j % 4) * 32, 32), 32)
                tok[2 * r + j // 4, to, :] = got.astype(BF)
            else:
                update_ref[at, :] = got

        if r:
            go(
                copy(
                    tok.at[pl.ds(2 * r, 2)],
                    tok.at[pl.ds(8 + 2 * r, 2)],
                    us.at[r],
                    ur.at[r],
                    dev(y, b, c, z),
                )
            )
    for r in (1, 3, 2):
        copy(tok.at[pl.ds(2 * r, 2)], tok.at[pl.ds(8 + 2 * r, 2)], us.at[r], ur.at[r], up).wait_recv()

        @pl.loop(0, 8)
        def _(j):
            at = pl.ds(pl.multiple_of(j * 32, 32), 32)
            to = pl.ds(pl.multiple_of((j % 4) * 32, 32), 32)
            update_ref[at, :] = update_ref[at, :] + tok[8 + 2 * r + j // 4, to, :].astype(F32)

    for cp in waits:
        cp.wait_send()


def local(out_grads, expert_ids, gate_probs, hidden_acts, q_previous):
    experts, rank, model = q_previous.shape
    hidden_units = hidden_acts.shape[3]
    width = model // lax.axis_size("dp")
    any_spec, vmem = pl.BlockSpec(memory_space=pl.ANY), pl.BlockSpec(memory_space=pltpu.VMEM)
    dma = lambda *shape: pltpu.SemaphoreType.DMA(shape)
    basis, update = pl.pallas_call(
        kernel,
        out_shape=(
            jax.ShapeDtypeStruct((experts * rank, hidden_units), F32),
            jax.ShapeDtypeStruct((experts * rank, width), F32),
        ),
        in_specs=[vmem, vmem, any_spec, any_spec, any_spec],
        out_specs=(vmem, vmem),
        scratch_shapes=[
            pltpu.VMEM((32, 128, width), BF),
            pltpu.VMEM((32, 16, 128), F32),
            pltpu.VMEM((4, 256, width), BF),
            pltpu.VMEM((32, 256, width), BF),
            pltpu.VMEM((512, 256), BF),
            pltpu.VMEM((512, 128), F32),
            pltpu.VMEM((8, 192, hidden_units), BF),
            pltpu.VMEM((4, 4, 64, 256), BF),
            pltpu.VMEM((4, 4, 64, 256), BF),
            pltpu.VMEM((256, 192), BF),
            pltpu.VMEM((4, 64, hidden_units), BF),
            pltpu.VMEM((4, 64, hidden_units), BF),
            pltpu.VMEM((128, hidden_units), F32),
            pltpu.VMEM((4, 64, hidden_units), BF),
            pltpu.VMEM((4, 64, 256), BF),
            pltpu.VMEM((4, 4, 64, 256), BF),
            dma(3),
            dma(4), dma(4), dma(2, 4), dma(2, 4), dma(2, 4), dma(2, 4), dma(4, 4), dma(4, 4),
            dma(4), dma(4), dma(2, 4), dma(2, 4), dma(4), dma(4), dma(4, 4), dma(4, 4),
            dma(4), dma(4), dma(4, 4), dma(4, 4), dma(4), dma(4), dma(4), dma(4),
            dma(4, 4), dma(4, 4), dma(4), dma(4),
        ],
        compiler_params=pltpu.CompilerParams(
            collective_id=0, has_side_effects=True, vmem_limit_bytes=67043328
        ),
    )(
        expert_ids[0].T,
        gate_probs[0].T,
        out_grads[0],
        hidden_acts[0],
        q_previous.reshape(experts * rank, model),
    )
    return (basis.reshape(experts, rank, hidden_units), update.reshape(experts, rank, width))


def solution(mesh):
    return jax.shard_map(
        local,
        mesh=mesh,
        in_specs=(
            P("dp", "expert", None),
            P("dp", "expert", None),
            P("dp", "expert", None),
            P("dp", "expert", None, None),
            P("expert", None, None),
        ),
        out_specs=(P("expert", None, None), P("expert", None, "dp")),
        check_vma=False,
    )
```

time: 639 us -> 197 us (0.31)
  the two profiles are of different devices: /device:TPU:6 before, /device:TPU:0 now
where the time goes in v1:
time: 197 us; the launch traced here: 196 us
  Pallas kernels  191 us (97%)
  local copies, waits for them, and re-layouts  4.5 us (2%)
    pallas_call x1, Pallas kernels, local(): pl.pallas_call(kernel, out_shape=(jax.ShapeDtypeStruct((experts * rank, h...  191 us
    unnamed x4, local copies, waits for them, and re-layouts  4.5 us

profile of v1, /device:TPU:0, one launch (start us, length us, event | category | flops | bytes accessed | tf_op | source)
XLA Modules:
  0.0 196.2 jit_solution(1467979610511852379)
XLA Ops:
  0.6 191.1 %shard_map.68 = (f32[256,2048]{1,0:T(8,128)}, f32[256,1792]{1,0:T(8,128)}) custom-call(s32[8,128]{1,0:T(8,128)} %bitcast.16, f32[8,128]{1,0:T(8,128)} %bitcast.17, bf16[128,7168]{1,0:T(8,128)(2,1)} %bitcast.14, bf16[8,192,2048]{2,1,0:T(8,128)(2,1)} %bitcast.11, bf16[256,7168]{1,0:T(8,128)(2,1)} %bitcast.12), custom_call_target="tpu_custom_call" | custom-call | tf_op jit(solution)/shard_map/pallas_call | solution.py:389
  191.7 0.0 copy-start
  191.7 3.3 %copy.9 = f32[8,32,2048]{2,1,0:T(8,128)} copy(f32[8,32,2048]{2,1,0:T(8,128)} %bitcast.13) | data formatting | bytes 4194304
  195.0 0.0 copy-done
  195.0 1.2 copy.10
Async XLA Ops:
  191.7 3.3 %copy-start = (f32[256,1792]{1,0:T(8,128)S(1)}, f32[256,1792]{1,0:T(8,128)}, u32[]{:S(2)}) copy-start(f32[256,1792]{1,0:T(8,128)} %get-tuple-element.5) | copy-start | bytes 5505028

commit v2 on v1

v2 whole, which is shorter than its diff:
```python
import math

import jax
import jax.numpy as jnp
from jax import lax
from jax.experimental import pallas as pl
from jax.experimental.pallas import tpu as pltpu
from jax.sharding import PartitionSpec as P

MESH = pl.DeviceIdType.MESH
BF, F32 = jnp.bfloat16, jnp.float32
HI = lax.Precision.HIGHEST
SLOT = 8
CAP = 6


def dot_nt(left, right, **more):
    return lax.dot_general(left, right, (((1,), (1,)), ((), ())), preferred_element_type=F32, **more)


def dot_nn(left, right, **more):
    return lax.dot_general(left, right, (((1,), (0,)), ((), ())), preferred_element_type=F32, **more)


def dot_tn(left, right, **more):
    return lax.dot_general(left, right, (((0,), (0,)), ((), ())), preferred_element_type=F32, **more)


def iota(shape, dim):
    return lax.broadcasted_iota(jnp.int32, shape, dim)


def kernel(
    ids_ref, gates_ref, grads_ref, hidden_ref, prev_ref, basis_ref, update_ref,
    tok, meta, q_row, routed, hid, m_out, m_in, m_t, hf, f_out, f_in, f_own, f_all, low, p_in, p_t,
    load_sem, zs, zr, as_, ar, hs, hr, ps, pr,
    mzs, mzr, mas, mar, mhs, mhr, mps, mpr,
    qs, qr, ms, mr, fs, fr, gs, gr, ls, lr, js, jr, us, ur,
):
    width = tok.shape[3]
    e, z = lax.axis_index("expert"), lax.axis_index("dp")
    y, x, c = e // 8, (e // 2) % 4, e % 2
    gather, spread = (y, x), (x, y)

    def turn(v, by):
        return lax.rem(v + by, 4)

    def dev(h, along_gather, along_spread, to_z, core=0):
        g, s = turn(gather[h], along_gather), turn(spread[h], along_spread)
        yy, xx = (g, s) if h == 0 else (s, g)
        cc = 1 - c if core else c
        return {"expert": (yy * 4 + xx) * 2 + cc, "dp": turn(z, to_z)}

    def copy(src, dst, send, recv, device):
        return pltpu.make_async_remote_copy(src, dst, send, recv, device_id=device, device_id_type=MESH)

    def block(zz, gg, cc):
        return (zz * 4 + gg) * 2 + cc

    def cols(zz, h):
        return pl.ds(pl.multiple_of(zz * (2 * width) + h * width, 128), width)

    own = [block(z, gather[h], c) for h in range(2)]
    load_tok = [
        pltpu.make_async_copy(grads_ref.at[:, cols(z, h)], tok.at[h, own[h]], load_sem.at[h])
        for h in range(2)
    ]
    load_q = [
        pltpu.make_async_copy(prev_ref.at[:, cols(z, h)], q_row.at[h, spread[h]], load_sem.at[2 + h])
        for h in range(2)
    ]
    load_hid = pltpu.make_async_copy(hidden_ref, hid, load_sem.at[4])
    for cp in load_tok + load_q + [load_hid]:
        cp.start()

    barrier = pltpu.get_barrier_semaphore()
    peers = [dev(0, 0, 0, 0, core=1)] + [dev(0, 0, 0, r) for r in (1, 2, 3)]
    for h in range(2):
        for b in (1, 2, 3):
            for r in range(4):
                peers.append(dev(h, 0, b, r))
    for peer in peers:
        pl.semaphore_signal(barrier, inc=1, device_id=peer, device_id_type=MESH)

    ids = ids_ref[...]
    expert_row = iota((256, 128), 0)
    named = jnp.zeros((256, 128), F32)
    for k in range(8):
        named = named + jnp.where(ids[k : k + 1, :] == expert_row, 1.0, 0.0)
    before = jnp.where(iota((128, 128), 0) < iota((128, 128), 1), 1.0, 0.0).astype(BF)
    earlier = dot_nn(named.astype(BF), before)
    place = jnp.concatenate(
        [
            jnp.sum(jnp.where(ids[k : k + 1, :] == expert_row, earlier, 0.0), axis=0, keepdims=True)
            for k in range(8)
        ],
        axis=0,
    )
    holder, inner = ids // 8, ids % 8
    at_y, at_x, at_c = holder // 8, (holder // 2) % 4, holder % 2
    for h, (g, s) in enumerate(((at_y, at_x), (at_x, at_y))):
        base = (g * 2 + at_c) * 256 + (s * 8 + inner) * SLOT
        meta[h, own[h], 0:8, :] = base.astype(F32) + place
        meta[h, own[h], 8:16, :] = gates_ref[...]

    pl.semaphore_wait(barrier, len(peers))

    waits = []

    def go(cp):
        cp.start()
        waits.append(cp)

    zorder = [0, 1, 3, 2]
    for r in (1, 3, 2):
        for h in range(2):
            b = own[h]
            to = turn(z, r)
            go(copy(meta.at[h, b], meta.at[h, b], mzs.at[h, r], mzr.at[h, r], dev(0, 0, 0, r)))
            go(copy(grads_ref.at[:, cols(to, h)], tok.at[h, b], zs.at[h, r], zr.at[h, r], dev(0, 0, 0, r)))

    partner = dev(0, 0, 0, 0, core=1)

    def to_partner(h, k, zz, dg):
        b = block(zz, turn(gather[h], dg), c)
        go(copy(meta.at[h, b], meta.at[h, b], mps.at[h, k, dg], mpr.at[h, k, dg], partner))
        go(copy(tok.at[h, b], tok.at[h, b], ps.at[h, k, dg], pr.at[h, k, dg], partner))

    def source(k):
        return turn(z, zorder[k])

    def stage_a(k):
        zz = source(k)
        for h in range(2):
            b = block(zz, gather[h], c)
            if k:
                r = (4 - zorder[k]) % 4
                copy(meta.at[h, b], meta.at[h, b], mzs.at[h, r], mzr.at[h, r], partner).wait_recv()
                copy(tok.at[h, b], tok.at[h, b], zs.at[h, r], zr.at[h, r], partner).wait_recv()
            else:
                load_tok[h].wait()
            for way, step in ((0, 1), (1, 3)):
                device = dev(h, step, 0, 0)
                go(copy(meta.at[h, b], meta.at[h, b], mas.at[h, way, k], mar.at[h, way, k], device))
                go(copy(tok.at[h, b], tok.at[h, b], as_.at[h, way, k], ar.at[h, way, k], device))
            to_partner(h, k, zz, 0)

    def stage_b(k):
        zz = source(k)
        for h in range(2):
            for way, step, dg in ((0, 1, 3), (1, 3, 1)):
                device = dev(h, step, 0, 0)
                b = block(zz, turn(gather[h], dg), c)
                copy(meta.at[h, b], meta.at[h, b], mas.at[h, way, k], mar.at[h, way, k], device).wait_recv()
                copy(tok.at[h, b], tok.at[h, b], as_.at[h, way, k], ar.at[h, way, k], device).wait_recv()
                half = pl.ds(way * 64, 64)
                if way == 0:
                    go(copy(meta.at[h, b], meta.at[h, b], mhs.at[h, k], mhr.at[h, k], device))
                go(copy(tok.at[h, b, half], tok.at[h, b, half], hs.at[h, way, k], hr.at[h, way, k], device))
                to_partner(h, k, zz, dg)

    def stage_h(k):
        zz = source(k)
        for h in range(2):
            b = block(zz, turn(gather[h], 2), c)
            copy(meta.at[h, b], meta.at[h, b], mhs.at[h, k], mhr.at[h, k], partner).wait_recv()
            for way in range(2):
                half = pl.ds(way * 64, 64)
                copy(
                    tok.at[h, b, half], tok.at[h, b, half], hs.at[h, way, k], hr.at[h, way, k], partner
                ).wait_recv()
            to_partner(h, k, zz, 2)

    mine = [((gather[h] * 2 + c) * 256).astype(F32) for h in range(2)]
    row_of = iota((256, 128), 0).astype(F32)
    chunks = [(n, min(256, width - n)) for n in range(0, width, 256)]

    def rows_of(h, zz, gg):
        pair = zz * 4 + gg
        less = jnp.where(h == 0, mine[0], mine[1])
        picks, scales = [], []
        for cc in range(2):
            info = meta[h, pair * 2 + cc]
            want = info[0:8] - less
            gate = jnp.zeros((256, 128), F32)
            for k in range(8):
                gate = jnp.where(row_of == want[k : k + 1], info[8 + k : 9 + k], gate)
            picks.append(jnp.where(gate > 0.0, 1.0, 0.0).astype(BF))
            scales.append(jnp.sum(gate, axis=1, keepdims=True))
        to = pl.ds(pl.multiple_of(pair * 16, 16), 16)
        for n, size in chunks:
            got = [
                (dot_nn(picks[cc], tok[h, pair * 2 + cc, :, n : n + size]) * scales[cc]).reshape(32, 8, size)
                for cc in range(2)
            ]
            routed[h, :, to, n : n + size] = jnp.concatenate(got, axis=1).astype(BF)

    lane_expert = iota((64, 256), 1) // 32

    def wait_partner(k, dg):
        zz = source(k)
        for h in range(2):
            b = block(zz, turn(gather[h], dg), 1 - c)
            copy(meta.at[h, b], meta.at[h, b], mps.at[h, k, dg], mpr.at[h, k, dg], partner).wait_recv()
            copy(tok.at[h, b], tok.at[h, b], ps.at[h, k, dg], pr.at[h, k, dg], partner).wait_recv()

    def stage_c(k):
        zz = source(k)
        for dg in (0, 1, 3):
            wait_partner(k, dg)

        @pl.loop(0, 6)
        def _(i):
            h, n = i % 2, i // 2
            rows_of(h, zz, turn(jnp.where(h == 0, y, x), n + n // 2))

        wait_partner(k, 2)

        @pl.loop(0, 2)
        def _(h):
            rows_of(h, zz, turn(jnp.where(h == 0, y, x), 2))

        part = pl.ds(pl.multiple_of(zz * 64, 64), 64)
        for h in range(2):
            for r in (2, 1, 3, 0):
                to = turn(spread[h], r)
                rows = routed[h, pl.ds(to * 8, 8), part, :].reshape(512, width)
                every = dot_nt(rows, q_row[h, to])
                total = jnp.zeros((64, 256), F32)
                for j in range(8):
                    total = total + jnp.where(lane_expert == j, every[j * 64 : j * 64 + 64], 0.0)
                if k == 0 and r == 0:
                    m_in[h, 0, 0] = total.astype(BF)
                else:
                    m_out[h, k, r] = total.astype(BF)
                    go(
                        copy(
                            m_out.at[h, k, r], m_in.at[h, r, k], ms.at[h, k, r], mr.at[h, k, r],
                            dev(h, 0, r, zorder[k]),
                        )
                    )

    stage_a(0)
    for h in range(2):
        load_q[h].wait()
        b = spread[h]
        for r in (2, 1, 3):
            go(copy(q_row.at[h, b], q_row.at[h, b], qs.at[h, r], qr.at[h, r], dev(h, 0, r, 0)))
    stage_a(1)
    stage_b(0)
    stage_a(2)
    stage_h(0)
    stage_b(1)
    for h in range(2):
        for r in (1, 2, 3):
            b = turn(spread[h], 4 - r)
            copy(q_row.at[h, b], q_row.at[h, b], qs.at[h, r], qr.at[h, r], partner).wait_recv()
    stage_c(0)
    stage_a(3)
    stage_h(1)
    stage_b(2)
    stage_c(1)
    stage_h(2)
    stage_b(3)
    stage_c(2)
    stage_h(3)
    stage_c(3)

    while waits:
        waits.pop(0).wait_send()

    load_hid.wait()

    def selection(h):
        row, slot = iota((256, 192), 0), iota((256, 192), 1)
        back = turn(spread[h] + 4 - row // 64, 0)
        along = (row // 16) % 4
        yy, xx = (along, back) if h == 0 else (back, along)
        at = ((yy * 4 + xx) * 2 + (row // 8) % 2) * CAP + row % 8
        return jnp.where((at == slot) & (row % 8 < CAP), 1.0, 0.0).astype(BF)

    select = [selection(h) for h in range(2)]
    mixed = jnp.zeros((256, 192), F32)
    for h in range(2):
        parts = []
        for r in range(4):
            total = None
            for k in range(4):
                if k or r:
                    copy(
                        m_out.at[h, k, r], m_in.at[h, r, k], ms.at[h, k, r], mr.at[h, k, r], partner
                    ).wait_recv()
                got = m_in[h, r, k].astype(F32)
                total = got if total is None else total + got
            parts.append(total)
        raw = jnp.concatenate(parts, axis=0)
        top = raw.astype(BF)
        rest = (raw - top.astype(F32)).astype(BF)
        mixed = mixed + dot_tn(top, select[h]) + dot_tn(rest, select[h])
    m_t[...] = mixed.astype(BF)

    for r in (2, 1, 3, 0):
        to = turn(z, r)
        for i in range(2):
            j = to * 2 + i
            rows = m_t[pl.ds(pl.multiple_of(j * 32, 32), 32), :]
            got = dot_nn(rows, hid[j])
            if r:
                f_out[r, i * 32 : i * 32 + 32, :] = got.astype(BF)
            else:
                f_own[i * 32 : i * 32 + 32, :] = got
        if r:
            go(copy(f_out.at[r], f_in.at[r], fs.at[r], fr.at[r], dev(0, 0, 0, r)))
    total = f_own[...]
    for r in (1, 3, 2):
        copy(f_out.at[r], f_in.at[r], fs.at[r], fr.at[r], partner).wait_recv()
        total = total + f_in[r].astype(F32)
    f_all[z] = total.astype(BF)
    for r in (2, 1, 3):
        go(copy(f_all.at[z], f_all.at[z], gs.at[r], gr.at[r], dev(0, 0, 0, r)))

    mat = f_all[z]
    gram = dot_nt(mat, jnp.concatenate([mat, mat], axis=0))
    lane, row = iota((32, 128), 1), iota((32, 128), 0)
    eye = jnp.where(lane % 32 == row, 1.0, 0.0)
    work = jnp.where(lane >= 96, gram[32:64], jnp.where(lane >= 64, gram[0:32], eye))
    first = (lane // 32) % 2 == 0
    for k in range(32):
        one = work[:, 64 + k : 65 + k]
        two = work[:, 96 + k : 97 + k]
        factor = jnp.where(first, one / one[k : k + 1, :], two / two[k : k + 1, :])
        factor = jnp.where(row > k, factor, 0.0)
        work = work - factor * work[k : k + 1, :]
    one = jnp.sum(jnp.where(lane == 64 + row, work, 0.0), axis=1, keepdims=True)
    two = jnp.sum(jnp.where(lane == 96 + row, work, 0.0), axis=1, keepdims=True)
    low[z] = work * jnp.where(first, 1.0 / jnp.sqrt(one), 1.0 / jnp.sqrt(two))
    for r in (2, 1, 3):
        go(copy(low.at[z], low.at[z], ls.at[r], lr.at[r], dev(0, 0, 0, r)))

    for r in (0, 1, 3, 2):
        zz = turn(z, 4 - r)
        if r:
            copy(f_all.at[zz], f_all.at[zz], gs.at[r], gr.at[r], partner).wait_recv()
        for i in range(2):
            j = zz * 2 + i
            got = dot_nt(f_all[zz, i * 32 : i * 32 + 32, :], hid[j])
            hf[pl.ds(pl.multiple_of(j * 32, 32), 32), :] = got
    place64 = iota((32, 64), 1) < 32

    def lower(zz):
        both = low[zz][:, 0:64]
        return jnp.concatenate([jnp.where(place64, both, 0.0), jnp.where(place64, 0.0, both)], axis=0)

    for r in (0, 1, 3, 2):
        zz = turn(z, 4 - r)
        if r:
            copy(low.at[zz], low.at[zz], ls.at[r], lr.at[r], partner).wait_recv()
        at = pl.ds(pl.multiple_of(zz * 64, 64), 64)
        m_t[at, :] = dot_nn(lower(zz), hf[at, :], precision=HI).astype(BF)
    while waits:
        waits.pop(0).wait_send()
    for h in range(2):
        spreads = dot_nt(select[h], m_t[...]).astype(BF)
        for r in range(4):
            m_out[h, 0, r] = spreads[r * 64 : r * 64 + 64]
        p_in[h, 0, z] = spreads[0:64]
        for r in (2, 1, 3, 0):
            for q in (2, 1, 3, 0):
                if r or q:
                    go(
                        copy(
                            m_out.at[h, 0, r], p_in.at[h, r, z], js.at[h, r, q], jr.at[h, r, q],
                            dev(h, 0, 4 - r, q),
                        )
                    )
    for zz in range(4):
        mat = lower(zz)
        top = mat.astype(BF)
        rest = (mat - top.astype(F32)).astype(BF)
        basis_ref[zz * 64 : zz * 64 + 64, :] = (dot_nn(top, f_all[zz]) + dot_nn(rest, f_all[zz])).astype(BF)

    for r in (2, 1, 3, 0):
        for h in range(2):
            b = turn(spread[h], r)
            for q in range(4):
                if r or q:
                    zz = turn(z, 4 - q)
                    copy(m_out.at[h, 0, r], p_in.at[h, r, zz], js.at[h, r, q], jr.at[h, r, q], partner).wait_recv()
            terms = jnp.concatenate([p_in[h, r, zz] for zz in range(4)], axis=0)
            p_t[...] = terms.astype(F32).T.astype(BF)

            @pl.loop(0, 8)
            def _(j):
                at = pl.ds(pl.multiple_of(j * 32, 32), 32)
                got = dot_nn(p_t[at, :], routed[h, b * 8 + j])
                if r:
                    to = pl.ds(pl.multiple_of((j % 4) * 32, 32), 32)
                    tok[h, 2 * r + j // 4, to, :] = got.astype(BF)
                else:
                    update_ref[at, h * width : h * width + width] = got

            if r:
                go(
                    copy(
                        tok.at[h, pl.ds(2 * r, 2)], tok.at[h, pl.ds(8 + 2 * r, 2)], us.at[h, r], ur.at[h, r],
                        dev(h, 0, r, 0),
                    )
                )
    for r in (1, 3, 2):
        for h in range(2):
            copy(
                tok.at[h, pl.ds(2 * r, 2)], tok.at[h, pl.ds(8 + 2 * r, 2)], us.at[h, r], ur.at[h, r], partner
            ).wait_recv()

            @pl.loop(0, 8)
            def _(j):
                at = pl.ds(pl.multiple_of(j * 32, 32), 32)
                to = pl.ds(pl.multiple_of((j % 4) * 32, 32), 32)
                side = slice(h * width, h * width + width)
                update_ref[at, side] = update_ref[at, side] + tok[h, 8 + 2 * r + j // 4, to, :].astype(F32)

    for cp in waits:
        cp.wait_send()


def local(out_grads, expert_ids, gate_probs, hidden_acts, q_previous):
    experts, rank, model = q_previous.shape
    hidden_units = hidden_acts.shape[3]
    width = model // lax.axis_size("dp")
    half = width // 2
    any_spec, vmem = pl.BlockSpec(memory_space=pl.ANY), pl.BlockSpec(memory_space=pltpu.VMEM)
    dma = lambda *shape: pltpu.SemaphoreType.DMA(shape)
    basis, update = pl.pallas_call(
        kernel,
        out_shape=(
            jax.ShapeDtypeStruct((experts * rank, hidden_units), BF),
            jax.ShapeDtypeStruct((experts * rank, width), F32),
        ),
        in_specs=[vmem, vmem, any_spec, any_spec, any_spec],
        out_specs=(vmem, vmem),
        scratch_shapes=[
            pltpu.VMEM((2, 32, 128, half), BF),
            pltpu.VMEM((2, 32, 16, 128), F32),
            pltpu.VMEM((2, 4, 256, half), BF),
            pltpu.VMEM((2, 32, 256, half), BF),
            pltpu.VMEM((8, 192, hidden_units), BF),
            pltpu.VMEM((2, 4, 4, 64, 256), BF),
            pltpu.VMEM((2, 4, 4, 64, 256), BF),
            pltpu.VMEM((256, 192), BF),
            pltpu.VMEM((256, 192), F32),
            pltpu.VMEM((4, 64, hidden_units), BF),
            pltpu.VMEM((4, 64, hidden_units), BF),
            pltpu.VMEM((64, hidden_units), F32),
            pltpu.VMEM((4, 64, hidden_units), BF),
            pltpu.VMEM((4, 32, 128), F32),
            pltpu.VMEM((2, 4, 4, 64, 256), BF),
            pltpu.VMEM((256, 256), BF),
            dma(5),
            dma(2, 4), dma(2, 4), dma(2, 2, 4), dma(2, 2, 4), dma(2, 2, 4), dma(2, 2, 4), dma(2, 4, 4), dma(2, 4, 4),
            dma(2, 4), dma(2, 4), dma(2, 2, 4), dma(2, 2, 4), dma(2, 4), dma(2, 4), dma(2, 4, 4), dma(2, 4, 4),
            dma(2, 4), dma(2, 4), dma(2, 4, 4), dma(2, 4, 4), dma(4), dma(4), dma(4), dma(4), dma(4), dma(4),
            dma(2, 4, 4), dma(2, 4, 4), dma(2, 4), dma(2, 4),
        ],
        compiler_params=pltpu.CompilerParams(
            collective_id=0, has_side_effects=True, vmem_limit_bytes=67043328
        ),
    )(
        expert_ids[0].T,
        gate_probs[0].T,
        out_grads[0],
        hidden_acts[0],
        q_previous.reshape(experts * rank, model),
    )
    basis = basis.reshape(experts, rank, hidden_units).astype(F32) * math.sqrt(hidden_units)
    return (basis, update.reshape(experts, rank, width))


def solution(mesh):
    return jax.shard_map(
        local,
        mesh=mesh,
        in_specs=(
            P("dp", "expert", None),
            P("dp", "expert", None),
            P("dp", "expert", None),
            P("dp", "expert", None, None),
            P("expert", None, None),
        ),
        out_specs=(P("expert", None, None), P("expert", None, "dp")),
        check_vma=False,
    )
```

time: 197 us -> 159 us (0.81)
  Pallas kernels: 191 us -> 154 us
  local copies, waits for them, and re-layouts: 4.5 us -> 1.23 us
  other arithmetic: 0 us -> 2.93 us
    pallas_call x1, Pallas kernels: 191 us -> 154 us  [local(): pl.pallas_call(kernel, out_shape=(jax.ShapeDtypeStruct((experts * rank, h...]
    unnamed x4 -> x3, local copies, waits for them, and re-layouts: 4.5 us -> 1.23 us
    mul x0 -> x1, other arithmetic: none -> 2.93 us  [local(): basis.reshape(experts, rank, hidden_units).astype(F32)]
where the time goes in v2:
time: 159 us
  Pallas kernels  154 us (97%)
  other arithmetic  2.93 us (2%)
    pallas_call x1, Pallas kernels, local(): pl.pallas_call(kernel, out_shape=(jax.ShapeDtypeStruct((experts * rank, h...  154 us

profile of v2, /device:TPU:0, one launch (start us, length us, event | category | flops | bytes accessed | tf_op | source)
XLA Modules:
  0.0 158.7 jit_solution(17601790983846546009)
XLA Ops:
  0.6 153.9 %shard_map.68 = (bf16[256,2048]{1,0:T(8,128)(2,1)}, f32[256,1792]{1,0:T(8,128)}) custom-call(s32[8,128]{1,0:T(8,128)} %bitcast.16, f32[8,128]{1,0:T(8,128)} %bitcast.17, bf16[128,7168]{1,0:T(8,128)(2,1)} %bitcast.14, bf16[8,192,2048]{2,1,0:T(8,128)(2,1)} %bitcast.11, bf16[256,7168]{1,0:T(8,128)(2,1)} %bitcast.12), custom_call_target="tpu_custom_call" | custom-call | tf_op jit(solution)/shard_map/pallas_call | solution.py:433
  154.5 0.0 copy-start
  154.5 2.9 %convert_multiply_fusion = f32[256,2048]{1,0:T(8,128)} fusion(bf16[256,2048]{1,0:T(8,128)(2,1)} %get-tuple-element.4), kind=kLoop, calls=%fused_computation | loop fusion | flops 1048576 | bytes 3145728 | tf_op jit(solution)/shard_map/mul | solution.py:474
  157.4 0.0 copy-done
  157.4 1.2 copy.8
Async XLA Ops:
  154.5 2.9 %copy-start = (f32[256,1792]{1,0:T(8,128)S(1)}, f32[256,1792]{1,0:T(8,128)}, u32[]{:S(2)}) copy-start(f32[256,1792]{1,0:T(8,128)} %get-tuple-element.5) | copy-start | bytes 5505028

commit v3 on v2

--- a/solution.py
+++ b/solution.py
@@ -111,7 +111,12 @@
         cp.start()
         waits.append(cp)
 
-    zorder = [0, 1, 3, 2]
+    zorder = [1, 3, 2, 0]
+    for h in range(2):
+        load_q[h].wait()
+        b = spread[h]
+        for way in range(2):
+            go(copy(q_row.at[h, b], q_row.at[h, b], qs.at[h, way], qr.at[h, way], dev(h, 0, 1 + 2 * way, 0)))
     for r in (1, 3, 2):
         for h in range(2):
             b = own[h]
@@ -133,7 +138,7 @@
         zz = source(k)
         for h in range(2):
             b = block(zz, gather[h], c)
-            if k:
+            if zorder[k]:
                 r = (4 - zorder[k]) % 4
                 copy(meta.at[h, b], meta.at[h, b], mzs.at[h, r], mzr.at[h, r], partner).wait_recv()
                 copy(tok.at[h, b], tok.at[h, b], zs.at[h, r], zr.at[h, r], partner).wait_recv()
@@ -204,7 +209,7 @@
             copy(meta.at[h, b], meta.at[h, b], mps.at[h, k, dg], mpr.at[h, k, dg], partner).wait_recv()
             copy(tok.at[h, b], tok.at[h, b], ps.at[h, k, dg], pr.at[h, k, dg], partner).wait_recv()
 
-    def stage_c(k):
+    def stage_rows(k):
         zz = source(k)
         for dg in (0, 1, 3):
             wait_partner(k, dg)
@@ -220,6 +225,8 @@
         def _(h):
             rows_of(h, zz, turn(jnp.where(h == 0, y, x), 2))
 
+    def stage_mix(k):
+        zz = source(k)
         part = pl.ds(pl.multiple_of(zz * 64, 64), 64)
         for h in range(2):
             for r in (2, 1, 3, 0):
@@ -229,8 +236,8 @@
                 total = jnp.zeros((64, 256), F32)
                 for j in range(8):
                     total = total + jnp.where(lane_expert == j, every[j * 64 : j * 64 + 64], 0.0)
-                if k == 0 and r == 0:
-                    m_in[h, 0, 0] = total.astype(BF)
+                if zorder[k] == 0 and r == 0:
+                    m_in[h, 0, k] = total.astype(BF)
                 else:
                     m_out[h, k, r] = total.astype(BF)
                     go(
@@ -240,31 +247,44 @@
                         )
                     )
 
+    for h in range(2):
+        for way, back in ((0, 3), (1, 1)):
+            b = turn(spread[h], back)
+            copy(q_row.at[h, b], q_row.at[h, b], qs.at[h, way], qr.at[h, way], partner).wait_recv()
+            part = pl.ds(way * 128, 128)
+            go(
+                copy(
+                    q_row.at[h, b, part], q_row.at[h, b, part], qs.at[h, 2 + way], qr.at[h, 2 + way],
+                    dev(h, 0, 1 + 2 * way, 0),
+                )
+            )
     stage_a(0)
-    for h in range(2):
-        load_q[h].wait()
-        b = spread[h]
-        for r in (2, 1, 3):
-            go(copy(q_row.at[h, b], q_row.at[h, b], qs.at[h, r], qr.at[h, r], dev(h, 0, r, 0)))
     stage_a(1)
     stage_b(0)
     stage_a(2)
     stage_h(0)
     stage_b(1)
-    for h in range(2):
-        for r in (1, 2, 3):
-            b = turn(spread[h], 4 - r)
-            copy(q_row.at[h, b], q_row.at[h, b], qs.at[h, r], qr.at[h, r], partner).wait_recv()
-    stage_c(0)
     stage_a(3)
+    stage_rows(0)
     stage_h(1)
     stage_b(2)
-    stage_c(1)
+    for h in range(2):
+        b = turn(spread[h], 2)
+        for way in range(2):
+            part = pl.ds(way * 128, 128)
+            copy(
+                q_row.at[h, b, part], q_row.at[h, b, part], qs.at[h, 2 + way], qr.at[h, 2 + way], partner
+            ).wait_recv()
+    stage_mix(0)
+    stage_rows(1)
     stage_h(2)
     stage_b(3)
-    stage_c(2)
+    stage_mix(1)
+    stage_rows(2)
     stage_h(3)
-    stage_c(3)
+    stage_mix(2)
+    stage_rows(3)
+    stage_mix(3)
 
     while waits:
         waits.pop(0).wait_send()
@@ -286,7 +306,7 @@
         for r in range(4):
             total = None
             for k in range(4):
-                if k or r:
+                if zorder[k] or r:
                     copy(
                         m_out.at[h, k, r], m_in.at[h, r, k], ms.at[h, k, r], mr.at[h, k, r], partner
                     ).wait_recv()
@@ -357,6 +377,8 @@
             copy(low.at[zz], low.at[zz], ls.at[r], lr.at[r], partner).wait_recv()
         at = pl.ds(pl.multiple_of(zz * 64, 64), 64)
         m_t[at, :] = dot_nn(lower(zz), hf[at, :], precision=HI).astype(BF)
+    while waits:
+        waits.pop(0).wait_send()
     while waits:
         waits.pop(0).wait_send()
     for h in range(2):

time: 159 us -> 153 us (0.962)
  Pallas kernels: 154 us -> 148 us
    pallas_call x1, Pallas kernels: 154 us -> 148 us  [local(): pl.pallas_call(kernel, out_shape=(jax.ShapeDtypeStruct((experts * rank, h...]
where the time goes in v3:
time: 153 us
  Pallas kernels  148 us (97%)
  other arithmetic  2.93 us (2%)
    pallas_call x1, Pallas kernels, local(): pl.pallas_call(kernel, out_shape=(jax.ShapeDtypeStruct((experts * rank, h...  148 us

profile of v3, /device:TPU:0, one launch (start us, length us, event | category | flops | bytes accessed | tf_op | source)
XLA Modules:
  0.0 152.7 jit_solution(7847615634332695966)
XLA Ops:
  0.6 147.9 %shard_map.68 = (bf16[256,2048]{1,0:T(8,128)(2,1)}, f32[256,1792]{1,0:T(8,128)}) custom-call(s32[8,128]{1,0:T(8,128)} %bitcast.16, f32[8,128]{1,0:T(8,128)} %bitcast.17, bf16[128,7168]{1,0:T(8,128)(2,1)} %bitcast.14, bf16[8,192,2048]{2,1,0:T(8,128)(2,1)} %bitcast.11, bf16[256,7168]{1,0:T(8,128)(2,1)} %bitcast.12), custom_call_target="tpu_custom_call" | custom-call | tf_op jit(solution)/shard_map/pallas_call | solution.py:455
  148.5 0.0 copy-start
  148.5 2.9 %convert_multiply_fusion = f32[256,2048]{1,0:T(8,128)} fusion(bf16[256,2048]{1,0:T(8,128)(2,1)} %get-tuple-element.4), kind=kLoop, calls=%fused_computation | loop fusion | flops 1048576 | bytes 3145728 | tf_op jit(solution)/shard_map/mul | solution.py:496
  151.4 0.0 copy-done
  151.5 1.2 copy.8
Async XLA Ops:
  148.5 2.9 %copy-start = (f32[256,1792]{1,0:T(8,128)S(1)}, f32[256,1792]{1,0:T(8,128)}, u32[]{:S(2)}) copy-start(f32[256,1792]{1,0:T(8,128)} %get-tuple-element.5) | copy-start | bytes 5505028

commit v4 on v3

--- a/solution.py
+++ b/solution.py
@@ -319,28 +319,33 @@
         mixed = mixed + dot_tn(top, select[h]) + dot_tn(rest, select[h])
     m_t[...] = mixed.astype(BF)
 
-    for r in (2, 1, 3, 0):
-        to = turn(z, r)
-        for i in range(2):
-            j = to * 2 + i
-            rows = m_t[pl.ds(pl.multiple_of(j * 32, 32), 32), :]
-            got = dot_nn(rows, hid[j])
+    units = hid.shape[2] // 2
+    for u in range(2):
+        for r in (2, 1, 3, 0):
+            to = turn(z, r)
+            for i in range(2):
+                j = to * 2 + i
+                rows = m_t[pl.ds(pl.multiple_of(j * 32, 32), 32), :]
+                got = dot_nn(rows, hid[j, :, u * units : u * units + units])
+                if r:
+                    f_out[r, u, i * 32 : i * 32 + 32, :] = got.astype(BF)
+                else:
+                    f_own[u, i * 32 : i * 32 + 32, :] = got
             if r:
-                f_out[r, i * 32 : i * 32 + 32, :] = got.astype(BF)
-            else:
-                f_own[i * 32 : i * 32 + 32, :] = got
-        if r:
-            go(copy(f_out.at[r], f_in.at[r], fs.at[r], fr.at[r], dev(0, 0, 0, r)))
-    total = f_own[...]
-    for r in (1, 3, 2):
-        copy(f_out.at[r], f_in.at[r], fs.at[r], fr.at[r], partner).wait_recv()
-        total = total + f_in[r].astype(F32)
-    f_all[z] = total.astype(BF)
-    for r in (2, 1, 3):
-        go(copy(f_all.at[z], f_all.at[z], gs.at[r], gr.at[r], dev(0, 0, 0, r)))
-
-    mat = f_all[z]
-    gram = dot_nt(mat, jnp.concatenate([mat, mat], axis=0))
+                go(copy(f_out.at[r, u], f_in.at[r, u], fs.at[u, r], fr.at[u, r], dev(0, 0, 0, r)))
+    for u in range(2):
+        total = f_own[u]
+        for r in (1, 3, 2):
+            copy(f_out.at[r, u], f_in.at[r, u], fs.at[u, r], fr.at[u, r], partner).wait_recv()
+            total = total + f_in[r, u].astype(F32)
+        f_all[z, u] = total.astype(BF)
+        for r in (2, 1, 3):
+            go(copy(f_all.at[z, u], f_all.at[z, u], gs.at[u, r], gr.at[u, r], dev(0, 0, 0, r)))
+
+    gram = jnp.zeros((64, 128), F32)
+    for u in range(2):
+        mat = f_all[z, u]
+        gram = gram + dot_nt(mat, jnp.concatenate([mat, mat], axis=0))
     lane, row = iota((32, 128), 1), iota((32, 128), 0)
     eye = jnp.where(lane % 32 == row, 1.0, 0.0)
     work = jnp.where(lane >= 96, gram[32:64], jnp.where(lane >= 64, gram[0:32], eye))
@@ -357,14 +362,16 @@
     for r in (2, 1, 3):
         go(copy(low.at[z], low.at[z], ls.at[r], lr.at[r], dev(0, 0, 0, r)))
 
-    for r in (0, 1, 3, 2):
-        zz = turn(z, 4 - r)
-        if r:
-            copy(f_all.at[zz], f_all.at[zz], gs.at[r], gr.at[r], partner).wait_recv()
-        for i in range(2):
-            j = zz * 2 + i
-            got = dot_nt(f_all[zz, i * 32 : i * 32 + 32, :], hid[j])
-            hf[pl.ds(pl.multiple_of(j * 32, 32), 32), :] = got
+    for u in range(2):
+        for r in (0, 1, 3, 2):
+            zz = turn(z, 4 - r)
+            if r:
+                copy(f_all.at[zz, u], f_all.at[zz, u], gs.at[u, r], gr.at[u, r], partner).wait_recv()
+            for i in range(2):
+                j = zz * 2 + i
+                at = pl.ds(pl.multiple_of(j * 32, 32), 32)
+                got = dot_nt(f_all[zz, u, i * 32 : i * 32 + 32, :], hid[j, :, u * units : u * units + units])
+                hf[at, :] = hf[at, :] + got if u else got
     place64 = iota((32, 64), 1) < 32
 
     def lower(zz):
@@ -399,7 +406,9 @@
         mat = lower(zz)
         top = mat.astype(BF)
         rest = (mat - top.astype(F32)).astype(BF)
-        basis_ref[zz * 64 : zz * 64 + 64, :] = (dot_nn(top, f_all[zz]) + dot_nn(rest, f_all[zz])).astype(BF)
+        for u in range(2):
+            both = dot_nn(top, f_all[zz, u]) + dot_nn(rest, f_all[zz, u])
+            basis_ref[zz * 64 : zz * 64 + 64, u * units : u * units + units] = both.astype(BF)
 
     for r in (2, 1, 3, 0):
         for h in range(2):
@@ -470,17 +479,17 @@
             pltpu.VMEM((2, 4, 4, 64, 256), BF),
             pltpu.VMEM((256, 192), BF),
             pltpu.VMEM((256, 192), F32),
-            pltpu.VMEM((4, 64, hidden_units), BF),
-            pltpu.VMEM((4, 64, hidden_units), BF),
-            pltpu.VMEM((64, hidden_units), F32),
-            pltpu.VMEM((4, 64, hidden_units), BF),
+            pltpu.VMEM((4, 2, 64, hidden_units // 2), BF),
+            pltpu.VMEM((4, 2, 64, hidden_units // 2), BF),
+            pltpu.VMEM((2, 64, hidden_units // 2), F32),
+            pltpu.VMEM((4, 2, 64, hidden_units // 2), BF),
             pltpu.VMEM((4, 32, 128), F32),
             pltpu.VMEM((2, 4, 4, 64, 256), BF),
             pltpu.VMEM((256, 256), BF),
             dma(5),
             dma(2, 4), dma(2, 4), dma(2, 2, 4), dma(2, 2, 4), dma(2, 2, 4), dma(2, 2, 4), dma(2, 4, 4), dma(2, 4, 4),
             dma(2, 4), dma(2, 4), dma(2, 2, 4), dma(2, 2, 4), dma(2, 4), dma(2, 4), dma(2, 4, 4), dma(2, 4, 4),
-            dma(2, 4), dma(2, 4), dma(2, 4, 4), dma(2, 4, 4), dma(4), dma(4), dma(4), dma(4), dma(4), dma(4),
+            dma(2, 4), dma(2, 4), dma(2, 4, 4), dma(2, 4, 4), dma(2, 4), dma(2, 4), dma(2, 4), dma(2, 4), dma(4), dma(4),
             dma(2, 4, 4), dma(2, 4, 4), dma(2, 4), dma(2, 4),
         ],
         compiler_params=pltpu.CompilerParams(

time: 153 us -> 152 us (level)
  no operation moved by 1% of the time
where the time goes in v4:
time: 152 us
  Pallas kernels  147 us (97%)
  other arithmetic  2.93 us (2%)
    pallas_call x1, Pallas kernels, local(): pl.pallas_call(kernel, out_shape=(jax.ShapeDtypeStruct((experts * rank, h...  147 us

profile of v4, /device:TPU:0, one launch (start us, length us, event | category | flops | bytes accessed | tf_op | source)
XLA Modules:
  0.0 151.6 jit_solution(6211530389404304570)
XLA Ops:
  0.6 146.8 %shard_map.68 = (bf16[256,2048]{1,0:T(8,128)(2,1)}, f32[256,1792]{1,0:T(8,128)}) custom-call(s32[8,128]{1,0:T(8,128)} %bitcast.16, f32[8,128]{1,0:T(8,128)} %bitcast.17, bf16[128,7168]{1,0:T(8,128)(2,1)} %bitcast.14, bf16[8,192,2048]{2,1,0:T(8,128)(2,1)} %bitcast.11, bf16[256,7168]{1,0:T(8,128)(2,1)} %bitcast.12), custom_call_target="tpu_custom_call" | custom-call | tf_op jit(solution)/shard_map/pallas_call | solution.py:464
  147.5 0.0 copy-start
  147.5 2.9 %convert_multiply_fusion = f32[256,2048]{1,0:T(8,128)} fusion(bf16[256,2048]{1,0:T(8,128)(2,1)} %get-tuple-element.4), kind=kLoop, calls=%fused_computation | loop fusion | flops 1048576 | bytes 3145728 | tf_op jit(solution)/shard_map/mul | solution.py:505
  150.4 0.0 copy-done
  150.4 1.2 copy.8
Async XLA Ops:
  147.5 2.9 %copy-start = (f32[256,1792]{1,0:T(8,128)S(1)}, f32[256,1792]{1,0:T(8,128)}, u32[]{:S(2)}) copy-start(f32[256,1792]{1,0:T(8,128)} %get-tuple-element.5) | copy-start | bytes 5505028

commit v5 on v4

--- a/solution.py
+++ b/solution.py
@@ -319,8 +319,8 @@
         mixed = mixed + dot_tn(top, select[h]) + dot_tn(rest, select[h])
     m_t[...] = mixed.astype(BF)
 
-    units = hid.shape[2] // 2
-    for u in range(2):
+    units = hid.shape[2] // 4
+    for u in range(4):
         for r in (2, 1, 3, 0):
             to = turn(z, r)
             for i in range(2):
@@ -333,7 +333,7 @@
                     f_own[u, i * 32 : i * 32 + 32, :] = got
             if r:
                 go(copy(f_out.at[r, u], f_in.at[r, u], fs.at[u, r], fr.at[u, r], dev(0, 0, 0, r)))
-    for u in range(2):
+    for u in range(4):
         total = f_own[u]
         for r in (1, 3, 2):
             copy(f_out.at[r, u], f_in.at[r, u], fs.at[u, r], fr.at[u, r], partner).wait_recv()
@@ -343,7 +343,7 @@
             go(copy(f_all.at[z, u], f_all.at[z, u], gs.at[u, r], gr.at[u, r], dev(0, 0, 0, r)))
 
     gram = jnp.zeros((64, 128), F32)
-    for u in range(2):
+    for u in range(4):
         mat = f_all[z, u]
         gram = gram + dot_nt(mat, jnp.concatenate([mat, mat], axis=0))
     lane, row = iota((32, 128), 1), iota((32, 128), 0)
@@ -362,7 +362,7 @@
     for r in (2, 1, 3):
         go(copy(low.at[z], low.at[z], ls.at[r], lr.at[r], dev(0, 0, 0, r)))
 
-    for u in range(2):
+    for u in range(4):
         for r in (0, 1, 3, 2):
             zz = turn(z, 4 - r)
             if r:
@@ -406,7 +406,7 @@
         mat = lower(zz)
         top = mat.astype(BF)
         rest = (mat - top.astype(F32)).astype(BF)
-        for u in range(2):
+        for u in range(4):
             both = dot_nn(top, f_all[zz, u]) + dot_nn(rest, f_all[zz, u])
             basis_ref[zz * 64 : zz * 64 + 64, u * units : u * units + units] = both.astype(BF)
 
@@ -479,17 +479,17 @@
             pltpu.VMEM((2, 4, 4, 64, 256), BF),
             pltpu.VMEM((256, 192), BF),
             pltpu.VMEM((256, 192), F32),
-            pltpu.VMEM((4, 2, 64, hidden_units // 2), BF),
-            pltpu.VMEM((4, 2, 64, hidden_units // 2), BF),
-            pltpu.VMEM((2, 64, hidden_units // 2), F32),
-            pltpu.VMEM((4, 2, 64, hidden_units // 2), BF),
+            pltpu.VMEM((4, 4, 64, hidden_units // 4), BF),
+            pltpu.VMEM((4, 4, 64, hidden_units // 4), BF),
+            pltpu.VMEM((4, 64, hidden_units // 4), F32),
+            pltpu.VMEM((4, 4, 64, hidden_units // 4), BF),
             pltpu.VMEM((4, 32, 128), F32),
             pltpu.VMEM((2, 4, 4, 64, 256), BF),
             pltpu.VMEM((256, 256), BF),
             dma(5),
             dma(2, 4), dma(2, 4), dma(2, 2, 4), dma(2, 2, 4), dma(2, 2, 4), dma(2, 2, 4), dma(2, 4, 4), dma(2, 4, 4),
             dma(2, 4), dma(2, 4), dma(2, 2, 4), dma(2, 2, 4), dma(2, 4), dma(2, 4), dma(2, 4, 4), dma(2, 4, 4),
-            dma(2, 4), dma(2, 4), dma(2, 4, 4), dma(2, 4, 4), dma(2, 4), dma(2, 4), dma(2, 4), dma(2, 4), dma(4), dma(4),
+            dma(2, 4), dma(2, 4), dma(2, 4, 4), dma(2, 4, 4), dma(4, 4), dma(4, 4), dma(4, 4), dma(4, 4), dma(4), dma(4),
             dma(2, 4, 4), dma(2, 4, 4), dma(2, 4), dma(2, 4),
         ],
         compiler_params=pltpu.CompilerParams(

time: 152 us -> 150 us (0.987)
  Pallas kernels: 147 us -> 145 us
    pallas_call x1, Pallas kernels: 147 us -> 145 us  [local(): pl.pallas_call(kernel, out_shape=(jax.ShapeDtypeStruct((experts * rank, h...]
where the time goes in v5:
time: 150 us
  Pallas kernels  145 us (97%)
  other arithmetic  2.93 us (2%)
    pallas_call x1, Pallas kernels, local(): pl.pallas_call(kernel, out_shape=(jax.ShapeDtypeStruct((experts * rank, h...  145 us

profile of v5, /device:TPU:0, one launch (start us, length us, event | category | flops | bytes accessed | tf_op | source)
XLA Modules:
  0.0 150.1 jit_solution(10951716706470069990)
XLA Ops:
  0.6 145.3 %shard_map.68 = (bf16[256,2048]{1,0:T(8,128)(2,1)}, f32[256,1792]{1,0:T(8,128)}) custom-call(s32[8,128]{1,0:T(8,128)} %bitcast.16, f32[8,128]{1,0:T(8,128)} %bitcast.17, bf16[128,7168]{1,0:T(8,128)(2,1)} %bitcast.14, bf16[8,192,2048]{2,1,0:T(8,128)(2,1)} %bitcast.11, bf16[256,7168]{1,0:T(8,128)(2,1)} %bitcast.12), custom_call_target="tpu_custom_call" | custom-call | tf_op jit(solution)/shard_map/pallas_call | solution.py:464
  145.9 0.0 copy-start
  146.0 2.9 %convert_multiply_fusion = f32[256,2048]{1,0:T(8,128)} fusion(bf16[256,2048]{1,0:T(8,128)(2,1)} %get-tuple-element.4), kind=kLoop, calls=%fused_computation | loop fusion | flops 1048576 | bytes 3145728 | tf_op jit(solution)/shard_map/mul | solution.py:505
  148.9 0.0 copy-done
  148.9 1.2 copy.8
Async XLA Ops:
  145.9 2.9 %copy-start = (f32[256,1792]{1,0:T(8,128)S(1)}, f32[256,1792]{1,0:T(8,128)}, u32[]{:S(2)}) copy-start(f32[256,1792]{1,0:T(8,128)} %get-tuple-element.5) | copy-start | bytes 5505028
